TPU v7x, 32 devices: a whole 2x2x4 slice. The times are simulated.
32 devices in a mesh: ctx: 8 (over y, x, core), tp: 4 (over z).
Axes of the slice: x: 2, y: 2, z: 4, core: 2. Of those that a mesh axis runs over, the one named last changes fastest.
Arguments:
- tokens: bfloat16 [4096, 4096], P('ctx'), may hold values from -48 to 48
- w_query: bfloat16 [4096, 4096], P(None, 'tp'), may hold values from -0.09375 to 0.09375
- w_key: bfloat16 [4096, 4096], P(None, 'tp'), may hold values from -0.09375 to 0.09375
- w_value: bfloat16 [4096, 4096], P(None, 'tp'), may hold values from -0.09375 to 0.09375
- w_out: bfloat16 [4096, 4096], P('tp'), may hold values from -0.09375 to 0.09375
- block_doc: int32 [64], replicated, may hold values from 0 to 1, never falling along the last dimension, each value on 1 to 56 neighbouring positions
- grad_out: bfloat16 [4096, 4096], P('ctx', 'tp'), may hold values from -6 to 6
Outputs:
- output: bfloat16 [4096, 4096], P('ctx', 'tp')
- grad_tokens: bfloat16 [4096, 4096], P('ctx', 'tp')
- grad_query_weight: float32 [4096, 4096], P('ctx', 'tp')
- grad_key_weight: float32 [4096, 4096], P('ctx', 'tp')
- grad_value_weight: float32 [4096, 4096], P('ctx', 'tp')
- grad_out_weight: float32 [4096, 4096], P('tp', 'ctx')
Inputs may be any that keep to these rules, and one draw needn't show every extreme that they name: block_doc never falls along the blocks; each document covers 1 to 56 consecutive blocks.
All inputs are finite; a program needn't handle non-finite values.
Results may differ from a plain program's by a relative error of at most 0.024.
The roundings to bfloat16 on the way count: a program that leaves them out, or rounds other values in their place, can miss the bound.
Values may be sent and summed in bfloat16 or wider, within the bound.
A program may use at most 192 MiB of HBM per device.

v0:
```python
import math
import jax
import jax.numpy as jnp
from jax import lax
from jax.sharding import PartitionSpec as P

HDIM = 128
BLOCK = 64
big_negative = -1e30


def elementwise_product(pattern, left_side, right_side):
    return jnp.einsum(pattern, left_side, right_side, preferred_element_type=jnp.float32)


def attend(
    query_row_matrix,
    key_row_matrix,
    value_row_matrix,
    summary_key,
    summary_value,
    allowed,
    causal,
    score_scale_factor,
):
    near_scores = (
        elementwise_product("nqhd,nkhd->nhqk", query_row_matrix, key_row_matrix)
        * score_scale_factor
    )
    near_scores = jnp.where(causal[None, None], near_scores, big_negative)
    distant_score_matrix = (
        elementwise_product("yzxo,lxo->yzxl", query_row_matrix, summary_key) * score_scale_factor
    )
    distant_score_matrix = jnp.where(allowed[:, None, None, :], distant_score_matrix, big_negative)
    row_top = jnp.maximum(
        jnp.transpose(jnp.max(near_scores, axis=3), (0, 2, 1)),
        jnp.max(distant_score_matrix, axis=3),
    )
    near_exp = jnp.exp(near_scores - jnp.transpose(row_top, (0, 2, 1))[..., None])
    far_exp = jnp.exp(distant_score_matrix - row_top[..., None])
    denom_sum = jnp.transpose(jnp.sum(near_exp, axis=3), (0, 2, 1)) + jnp.sum(far_exp, axis=3)
    local_weight = (near_exp / jnp.transpose(denom_sum, (0, 2, 1))[..., None]).astype(jnp.bfloat16)
    distant_weight = (far_exp / denom_sum[..., None]).astype(jnp.bfloat16)
    combined_output = elementwise_product(
        "jvyb,jbvo->jyvo", local_weight, value_row_matrix
    ) + elementwise_product("gtuv,vuk->gtuk", distant_weight, summary_value)
    return (combined_output.astype(jnp.bfloat16), local_weight, distant_weight)


def attend_back(
    query_row_matrix,
    key_row_matrix,
    value_row_matrix,
    summary_key,
    summary_value,
    combined_output,
    local_weight,
    distant_weight,
    incoming_gradient,
    score_scale_factor,
):
    row_delta = jnp.sum(
        combined_output.astype(jnp.float32) * incoming_gradient.astype(jnp.float32), axis=3
    )
    near_d = elementwise_product("nqhd,nkhd->nhqk", incoming_gradient, value_row_matrix)
    distant_gradient_term = elementwise_product("yzxo,lxo->yzxl", incoming_gradient, summary_value)
    local_score_sum = (
        local_weight.astype(jnp.float32) * (near_d - jnp.transpose(row_delta, (0, 2, 1))[..., None])
    ).astype(jnp.bfloat16)
    distant_score_sum = (
        distant_weight.astype(jnp.float32) * (distant_gradient_term - row_delta[..., None])
    ).astype(jnp.bfloat16)
    query_gradient = (
        elementwise_product("jvyb,jbvo->jyvo", local_score_sum, key_row_matrix)
        + elementwise_product("gtuv,vuk->gtuk", distant_score_sum, summary_key)
    ) * score_scale_factor
    d_key = (
        elementwise_product("nhqk,nqhd->nkhd", local_score_sum, query_row_matrix)
        * score_scale_factor
    )
    d_value = elementwise_product("nhqk,nqhd->nkhd", local_weight, incoming_gradient)
    summary_key_gradient = (
        elementwise_product("agwi,agwu->iwu", distant_score_sum, query_row_matrix)
        * score_scale_factor
    )
    summary_value_gradient = elementwise_product(
        "agwi,agwu->iwu", distant_weight, incoming_gradient
    )
    return (query_gradient, d_key, d_value, summary_key_gradient, summary_value_gradient)


def back_project(grad_rows, weight):
    return lax.dot_general(
        grad_rows, weight, (((1,), (1,)), ((), ())), preferred_element_type=jnp.float32
    )


def term_maker(tokens, grad_rows):
    return lax.dot_general(
        tokens, grad_rows, (((0,), (0,)), ((), ())), preferred_element_type=jnp.float32
    )


def scatter_sum(partial, axis):
    count = lax.axis_size(axis)
    me = lax.axis_index(axis)
    width = partial.shape[1] // count

    def block(shift):
        return lax.dynamic_slice_in_dim(partial, (me + shift) % count * width, width, 1)

    total = block(0)
    for shift in range(1, count):
        ring = [(source, (source + shift) % count) for source in range(count)]
        moved = lax.ppermute(block(shift).astype(jnp.bfloat16), axis, ring)
        total = total + moved.astype(jnp.float32)
    return total


def per_device(tokens, w_query, w_key, w_value, w_out, block_doc, grad_out):
    score_scale_factor = 1.0 / math.sqrt(HDIM)
    tok_rows = tokens.shape[0]
    col_count = w_query.shape[1]
    blocks = tok_rows // BLOCK
    head_count = col_count // HDIM
    block_shape = (blocks, BLOCK, head_count, HDIM)

    def project(weight):
        return jnp.dot(tokens, weight, preferred_element_type=jnp.float32).astype(jnp.bfloat16)

    query_row_matrix = project(w_query).reshape(block_shape)
    key_row_matrix = project(w_key).reshape(block_shape)
    value_row_matrix = project(w_value).reshape(block_shape)
    own_key = key_row_matrix[:, BLOCK - 1].reshape(blocks, col_count)
    own_value = value_row_matrix[:, BLOCK - 1].reshape(blocks, col_count)
    summary = lax.all_gather(
        jnp.concatenate([own_key, own_value], axis=1), "ctx", axis=0, tiled=True
    )
    summary_key, summary_value = (summary[:, :col_count], summary[:, col_count:])
    total_blocks = summary_key.shape[0]
    summary_key = summary_key.reshape(total_blocks, head_count, HDIM)
    summary_value = summary_value.reshape(total_blocks, head_count, HDIM)
    first_block = lax.axis_index("ctx") * blocks
    query_ids = first_block + jnp.arange(blocks, dtype=jnp.int32)
    own_doc = lax.dynamic_slice_in_dim(block_doc, first_block, blocks, 0)
    block_ids = jnp.arange(total_blocks, dtype=jnp.int32)
    allowed = (block_ids[None, :] < query_ids[:, None]) & (block_doc[None, :] == own_doc[:, None])
    positions = jnp.arange(BLOCK, dtype=jnp.int32)
    causal = positions[None, :] <= positions[:, None]
    combined_output, local_weight, distant_weight = attend(
        query_row_matrix,
        key_row_matrix,
        value_row_matrix,
        summary_key,
        summary_value,
        allowed,
        causal,
        score_scale_factor,
    )
    attn = combined_output.reshape(tok_rows, col_count)
    partial_value = jnp.dot(attn, w_out, preferred_element_type=jnp.float32)
    summed = scatter_sum(partial_value, "tp")
    shard_width = summed.shape[1]
    residual = lax.dynamic_slice_in_dim(tokens, lax.axis_index("tp") * shard_width, shard_width, 1)
    output = (residual.astype(jnp.float32) + summed).astype(jnp.bfloat16)
    upstream_full = lax.all_gather(grad_out, "tp", axis=1, tiled=True)
    d_attn = back_project(upstream_full, w_out).astype(jnp.bfloat16)
    grads = attend_back(
        query_row_matrix,
        key_row_matrix,
        value_row_matrix,
        summary_key,
        summary_value,
        combined_output,
        local_weight,
        distant_weight,
        d_attn.reshape(block_shape),
        score_scale_factor,
    )
    query_gradient, d_key, d_value, summary_key_gradient, summary_value_gradient = grads
    flat_key = summary_key_gradient.reshape(total_blocks, col_count)
    flat_value = summary_value_gradient.reshape(total_blocks, col_count)
    back = lax.psum_scatter(
        jnp.concatenate([flat_key, flat_value], axis=1), "ctx", scatter_dimension=0, tiled=True
    )
    back_key, back_value = (back[:, :col_count], back[:, col_count:])
    query_gradient = query_gradient.astype(jnp.bfloat16).reshape(tok_rows, col_count)
    d_key = (
        d_key.at[:, BLOCK - 1]
        .add(back_key.reshape(blocks, head_count, HDIM))
        .astype(jnp.bfloat16)
        .reshape(tok_rows, col_count)
    )
    d_value = (
        d_value.at[:, BLOCK - 1]
        .add(back_value.reshape(blocks, head_count, HDIM))
        .astype(jnp.bfloat16)
        .reshape(tok_rows, col_count)
    )
    d_partial = (
        back_project(query_gradient, w_query)
        + back_project(d_key, w_key)
        + back_project(d_value, w_value)
    )
    d_summed = scatter_sum(d_partial, "tp")
    grad_tokens = (grad_out.astype(jnp.float32) + d_summed).astype(jnp.bfloat16)
    stacked = jnp.concatenate([query_gradient, d_key, d_value], axis=1)
    joined = lax.psum_scatter(
        term_maker(tokens, stacked).astype(jnp.bfloat16), "ctx", scatter_dimension=0, tiled=True
    ).astype(jnp.float32)
    grad_query_weight = joined[:, :col_count]
    grad_key_weight = joined[:, col_count : 2 * col_count]
    grad_value_weight = joined[:, 2 * col_count :]
    out_term = lax.dot_general(
        attn, upstream_full, (((0,), (0,)), ((), ())), preferred_element_type=jnp.float32
    )
    grad_out_weight = lax.psum_scatter(
        out_term.astype(jnp.bfloat16), "ctx", scatter_dimension=1, tiled=True
    ).astype(jnp.float32)
    return (
        output,
        grad_tokens,
        grad_query_weight,
        grad_key_weight,
        grad_value_weight,
        grad_out_weight,
    )


def solution(mesh):
    in_specs = (
        P("ctx", None),
        P(None, "tp"),
        P(None, "tp"),
        P(None, "tp"),
        P("tp", None),
        P(),
        P("ctx", "tp"),
    )
    out_specs = (
        P("ctx", "tp"),
        P("ctx", "tp"),
        P("ctx", "tp"),
        P("ctx", "tp"),
        P("ctx", "tp"),
        P("tp", "ctx"),
    )
    return jax.shard_map(
        per_device, mesh=mesh, in_specs=in_specs, out_specs=out_specs, check_vma=False
    )
```

profile of v0, /device:TPU:0, one launch (start us, length us, event | category | flops | bytes accessed | tf_op | source)
XLA Modules:
  0.0 398.2 jit_solution(12532342592921492758)
XLA Ops:
  7.2 0.7 all-gather.2.cloned.1.call-update
  8.0 9.3 %fusion.14 = bf16[64,8,8,128]{3,1,2,0:T(8,128)(2,1)S(1)} fusion(bf16[512,4096]{1,0:T(8,128)(2,1)} %param.11, bf16[4096,1024]{1,0:T(8,128)(2,1)} %param.12), kind=kOutput, calls=%fused_computation.41 | convolution fusion | flops 4295491584 | bytes 13631488 | tf_op jit(solution)/shard_map/dot_general | solution.py:129
  17.3 4.5 %fusion.15 = bf16[64,8,8,128]{3,1,2,0:T(8,128)(2,1)S(1)} fusion(bf16[512,4096]{1,0:T(8,128)(2,1)S(1)} %copy-done.18, bf16[4096,1024]{1,0:T(8,128)(2,1)S(1)} %copy-done.27), kind=kOutput, calls=%fused_computation.42 | convolution fusion | flops 4295491584 | bytes 13631488 | tf_op jit(solution)/shard_map/dot_general | solution.py:129
  22.3 9.5 %fusion.13 = bf16[64,8,8,128]{3,1,2,0:T(8,128)(2,1)S(1)} fusion(bf16[512,4096]{1,0:T(8,128)(2,1)} %param.11, bf16[4096,1024]{1,0:T(8,128)(2,1)} %param.14), kind=kOutput, calls=%fused_computation.40 | convolution fusion | flops 4295491584 | bytes 13631488 | tf_op jit(solution)/shard_map/dot_general | solution.py:129
  32.2 0.9 copy-done.12
  33.2 11.0 %all_gather.6 = bf16[64,2048]{1,0:T(8,128)(2,1)S(1)} all-gather(bf16[8,2048]{1,0:T(8,128)(2,1)S(1)} %pad_maximum_fusion.1), channel_id=1, replica_groups=mesh['ctx'=8,'tp'=4] {'ctx'}, dimensions={0}, use_global_device_ids=true | all-gather | bytes 294912 | tf_op jit(solution)/shard_map/all_gather | solution.py:136
  44.5 1.2 fusion.51
  45.7 0.7 fusion.10
  46.4 0.5 fusion.11
  47.0 0.7 fusion.12
  47.7 0.5 divide_convert_fusion
  48.3 0.6 copy-done.13
  48.9 2.1 fusion.29
  51.0 42.1 %all-gather.2.cloned.1.call-done = bf16[512,4096]{1,0:T(8,128)(2,1)} async-done(((bf16[512,1024]{1,0:T(8,128)(2,1)}), bf16[512,4096]{1,0:T(8,128)(2,1)}) %all-gather.2.cloned.1.call-update) | async-done | bytes 4194320 | tf_op jit(solution)/shard_map/all_gather | solution.py:166
  93.0 9.2 %fusion.16 = bf16[64,8,8,128]{3,1,2,0:T(8,128)(2,1)S(1)} fusion(bf16[512,4096]{1,0:T(8,128)(2,1)} %all-gather.2.cloned.1.call-done, bf16[1024,4096]{1,0:T(8,128)(2,1)} %param.15), kind=kOutput, calls=%fused_computation.43 | convolution fusion | flops 4295491584 | bytes 13631488 | tf_op jit(solution)/shard_map/dot_general | solution.py:93
  103.0 0.8 copy-done.11
  103.8 1.1 multiply_reduce_fusion
  104.9 1.7 copy.123
  106.6 1.1 fusion.8
  107.8 1.0 copy-done.5
  108.7 0.7 fusion.18
  109.4 0.9 pad_maximum_fusion
  110.4 9.0 %convolution_convert_fusion = bf16[1024,4096]{1,0:T(8,128)(2,1)} fusion(bf16[512,4096]{1,0:T(8,128)(2,1)} %all-gather.2.cloned.1.call-done, bf16[64,8,8,128]{3,2,1,0:T(8,128)(2,1)S(1)} %bitcast.187), kind=kOutput, calls=%fused_computation.2 | convolution fusion | flops 4299161600 | bytes 13631488 | tf_op jit(solution)/shard_map/dot_general | solution.py:214
  119.5 0.7 copy-done.21
  120.1 2.4 fusion.39
  122.6 1.3 copy-done.8
  123.9 1.0 multiply_convert_fusion
  125.6 0.7 copy-done.6
  126.4 0.5 fusion.6
  126.9 0.7 copy.135
  127.6 1.0 copy-done.2
  128.6 1.2 copy.258
  130.2 12.8 %reduce-scatter.4.cloned.1.call-done = f32[8,2048]{1,0:T(8,128)} async-done(((f32[64,2048]{1,0:T(8,128)}), f32[8,2048]{1,0:T(8,128)}) %reduce-scatter.4.cloned.1.call-update) | async-done | bytes 65552 | tf_op jit(solution)/shard_map/reduce_scatter | solution.py:183
  143.0 0.8 slice_bitcast_fusion.4
  143.8 1.7 scatter-add.9
  145.6 1.8 convert_element_type.135
  147.4 1.7 copy.144
  149.2 0.6 scatter-add.6
  150.0 0.7 copy.141
  151.5 1.6 copy-done.19
  153.0 0.6 copy-done.17
  153.6 18.3 %convert_bitcast_fusion = bf16[4096,3072]{0,1:T(8,128)(2,1)} fusion(bf16[512,4096]{1,0:T(8,128)(2,1)S(1)} %copy-done.19, bf16[512,1024]{1,0:T(8,128)(2,1)S(1)} %bitcast.191, bf16[512,1024]{1,0:T(8,128)(2,1)S(1)} %bitcast.190, bf16[512,1024]{1,0:T(8,128)(2,1)S(1)} %bitcast.189), kind=kOutput, calls=%fused_computation | convolution fusion | flops 12906921984 | bytes 32505856 | tf_op jit(solution)/shard_map/dot_general | solution.py:99
  172.0 1.3 copy-done.16
  173.3 10.1 %fusion.20 = f32[512,4096]{1,0:T(8,128)} fusion(bf16[1024,4096]{1,0:T(8,128)(2,1)} %param.15, bf16[64,8,8,128]{3,2,1,0:T(8,128)(2,1)S(1)} %bitcast.188), kind=kOutput, calls=%fused_computation.52 | convolution fusion | flops 4294967296 | bytes 17825792 | tf_op jit(solution)/shard_map/dot_general | solution.py:161
  183.3 5.0 %dynamic-slice_convert_fusion.5 = (bf16[512,1024]{1,0:T(8,128)(2,1)}, bf16[512,1024]{1,0:T(8,128)(2,1)}, bf16[512,1024]{1,0:T(8,128)(2,1)}) fusion(f32[512,4096]{1,0:T(8,128)} %fusion.20, s32[]{:T(128)S(6)} %select_n.64, s32[]{:T(128)S(6)} %select_n.68, s32[]{:T(128)S(6)} %select_n.66), kind=kLoop, calls=%fused_computation.27 | loop fusion | bytes 6291468 | tf_op jit(solution)/shard_map/convert_element_type | solution.py:115
  188.3 1.4 collective-permute-start
  189.7 2.5 collective-permute-start.2
  192.3 0.5 collective-permute-start.1
  192.8 10.5 %fusion.48 = f32[512,4096]{1,0:T(8,128)} fusion(bf16[4096,1024]{1,0:T(8,128)(2,1)} %param.12, bf16[64,8,8,128]{3,2,1,0:T(8,128)(2,1)S(1)} %bitcast.178), kind=kOutput, calls=%fused_computation.104 | convolution fusion | flops 4294967296 | bytes 17825792 | tf_op jit(solution)/shard_map/dot_general | solution.py:93
  203.3 6.8 %fusion.49 = f32[512,4096]{1,0:T(8,128)} fusion(bf16[4096,1024]{1,0:T(8,128)(2,1)S(1)} %bitcast.200, bf16[64,8,8,128]{3,2,1,0:T(8,128)(2,1)S(1)} %bitcast.182), kind=kOutput, calls=%fused_computation.105 | convolution fusion | flops 4294967296 | bytes 17825792 | tf_op jit(solution)/shard_map/dot_general | solution.py:93
  210.1 12.9 %add_add_fusion = f32[512,4096]{1,0:T(8,128)} fusion(f32[512,4096]{1,0:T(8,128)} %fusion.48, f32[512,4096]{1,0:T(8,128)} %fusion.49, bf16[4096,1024]{1,0:T(8,128)(2,1)} %param.14, bf16[64,8,8,128]{3,2,1,0:T(8,128)(2,1)S(1)} %bitcast.180), kind=kOutput, calls=%fused_computation.1 | convolution fusion | flops 4299161600 | bytes 34603008 | tf_op jit(solution)/shard_map/dot_general | solution.py:93
  223.0 4.3 %dynamic-slice_convert_fusion.2 = (bf16[512,1024]{1,0:T(8,128)(2,1)}, bf16[512,1024]{1,0:T(8,128)(2,1)S(1)}, bf16[512,1024]{1,0:T(8,128)(2,1)S(1)}) fusion(f32[512,4096]{1,0:T(8,128)} %add_add_fusion, s32[]{:T(128)S(6)} %select_n.64, s32[]{:T(128)S(6)} %select_n.68, s32[]{:T(128)S(6)} %select_n.66), kind=kLoop, calls=%fused_computation.20 | loop fusion | bytes 6291468 | tf_op jit(solution)/shard_map/convert_element_type | solution.py:115
  227.4 1.4 collective-permute-start.3
  228.7 2.5 collective-permute-start.5
  231.2 30.6 %collective-permute-start.4 = (bf16[512,1024]{1,0:T(8,128)(2,1)S(1)}, bf16[512,1024]{1,0:T(8,128)(2,1)}, u32[]{:S(2)}, u32[]{:S(2)}) collective-permute-start(bf16[512,1024]{1,0:T(8,128)(2,1)S(1)} %get-tuple-element.56), channel_id=1, source_target_pairs={{0,2},{1,3},{2,0},{3,1},{4,6},{5,7},{6,4},{7,5},{8,10},{9,11},{10,... | collective-permute-start | bytes 3145736 | tf_op jit(solution)/shard_map/ppermute | solution.py:115
  261.8 44.6 %collective-permute-done.1 = bf16[512,1024]{1,0:T(8,128)(2,1)} collective-permute-done((bf16[512,1024]{1,0:T(8,128)(2,1)}, bf16[512,1024]{1,0:T(8,128)(2,1)}, u32[]{:S(2)}, u32[]{:S(2)}) %collective-permute-start.1) | collective-permute-done | bytes 1048608 | tf_op jit(solution)/shard_map/ppermute | solution.py:115
  306.4 4.8 %add_convert_fusion.1 = bf16[512,1024]{1,0:T(8,128)(2,1)} fusion(bf16[512,1024]{1,0:T(8,128)(2,1)} %collective-permute-done.2, bf16[512,1024]{1,0:T(8,128)(2,1)} %collective-permute-done.1, bf16[512,1024]{1,0:T(8,128)(2,1)} %collective-permute-done, f32[512,4096]{1,0:T(8,128)} %fusion.20, s32[]{:T(128)S(6)} %select_n.62, bf16[512,4096]{1,0:T(8,128)(2,1)} %param.11, ...), kind=kLoop, calls=%fused_computation.24 | loop fusion | flops 4718592 | bytes 7340040 | tf_op jit(solution)/shard_map/convert_element_type | solution.py:165
  311.2 60.4 %collective-permute-done.4 = bf16[512,1024]{1,0:T(8,128)(2,1)} collective-permute-done((bf16[512,1024]{1,0:T(8,128)(2,1)S(1)}, bf16[512,1024]{1,0:T(8,128)(2,1)}, u32[]{:S(2)}, u32[]{:S(2)}) %collective-permute-start.4) | collective-permute-done | bytes 1048608 | tf_op jit(solution)/shard_map/ppermute | solution.py:115
  371.6 4.7 %add_convert_fusion = bf16[512,1024]{1,0:T(8,128)(2,1)} fusion(bf16[512,1024]{1,0:T(8,128)(2,1)} %collective-permute-done.5, bf16[512,1024]{1,0:T(8,128)(2,1)} %collective-permute-done.4, bf16[512,1024]{1,0:T(8,128)(2,1)} %collective-permute-done.3, f32[512,4096]{1,0:T(8,128)} %add_add_fusion, s32[]{:T(128)S(6)} %select_n.62, bf16[512,1024]{1,0:T(8,128)(2,1)S(1)} %copy-done.7), kind=kLoop, calls=%fused_computation.17 | loop fusion | flops 4718592 | bytes 7340036 | tf_op jit(solution)/shard_map/convert_element_type | solution.py:206
  376.3 2.9 convert_element_type.147
  379.2 4.8 %fusion.50 = (f32[512,1024]{0,1:T(8,128)}, f32[512,1024]{0,1:T(8,128)}, f32[512,1024]{0,1:T(8,128)S(1)}) fusion(bf16[512,3072]{0,1:T(8,128)(2,1)} %reduce-scatter.6.cloned.1.call-done), kind=kLoop, calls=%fused_computation.106 | loop fusion | bytes 12582912 | tf_op jit(solution)/shard_map/slice | solution.py:213
  383.9 2.9 copy.147
  386.8 2.9 copy.146
  389.7 1.8 copy.145
  (97 shorter events, 4.6 us)
Async XLA Ops:
  7.2 85.9 %all-gather.2.cloned.1.call-start = ((), (), s32[]{:S(2)}) async-start(), calls=%async_computation.3 | async-start | bytes 5242880 | tf_op jit(solution)/shard_map/all_gather | solution.py:166
  7.9 135.1 %reduce-scatter.4.cloned.1.call-start = ((), (), s32[]{:S(2)}) async-start(), calls=%async_computation.4 | async-start | bytes 589824 | tf_op jit(solution)/shard_map/reduce_scatter | solution.py:183
  7.9 9.3 %copy-start.18 = (bf16[512,4096]{1,0:T(8,128)(2,1)S(1)}, bf16[512,4096]{1,0:T(8,128)(2,1)}, u32[]{:S(2)}) copy-start(bf16[512,4096]{1,0:T(8,128)(2,1)} %param.11) | copy-start | bytes 12582916
  8.0 9.3 %copy-start.27 = (bf16[4096,1024]{1,0:T(8,128)(2,1)S(1)}, bf16[4096,1024]{1,0:T(8,128)(2,1)}, u32[]{:S(2)}) copy-start(bf16[4096,1024]{1,0:T(8,128)(2,1)} %param.13) | copy-start | bytes 25165828
  22.3 23.3 %copy-start = (bf16[64,8,8,128]{3,2,1,0:T(8,128)(2,1)}, bf16[64,8,8,128]{3,2,1,0:T(8,128)(2,1)S(1)}, u32[]{:S(2)}) copy-start(bf16[64,8,8,128]{3,2,1,0:T(8,128)(2,1)S(1)} %copy.169) | copy-start | bytes 3145732
  31.9 12.4 %copy-start.26 = (s32[64]{0:T(128)S(1)}, s32[64]{0:T(128)}, u32[]{:S(2)}) copy-start(s32[64]{0:T(128)} %param.16) | copy-start | bytes 772
  32.2 1.0 copy-start.12
  46.4 1.9 copy-start.9
  47.0 1.3 copy-start.20
  47.6 1.2 copy-start.13
  47.7 0.6 copy-start.24
  102.2 1.6 copy-start.11
  104.9 2.8 copy-start.22
  107.7 1.0 copy-start.5
  108.7 1.6 copy-start.15
  110.3 266.0 %reduce-scatter.8.cloned.1.call-start = ((), (), s32[]{:S(2)}) async-start(), calls=%async_computation.6 | async-start | bytes 9437184 | tf_op jit(solution)/shard_map/reduce_scatter | solution.py:217
  119.4 0.8 copy-start.21
  119.4 0.8 copy-start.25
  119.4 4.5 %copy-start.14 = (bf16[64,8,8,128]{3,2,1,0:T(8,128)(2,1)S(1)}, bf16[64,8,8,128]{3,2,1,0:T(8,128)(2,1)}, u32[]{:S(2)}) copy-start(bf16[64,8,8,128]{3,2,1,0:T(8,128)(2,1)} %copy-done.12) | copy-start | bytes 3145732
  119.4 4.5 %copy-start.23 = (f32[8,64,8]{1,2,0:T(8,128)S(1)}, f32[8,64,8]{1,2,0:T(8,128)}, u32[]{:S(2)}) copy-start(f32[8,64,8]{1,2,0:T(8,128)} %copy-done.22) | copy-start | bytes 49156
  119.4 259.8 %reduce-scatter.6.cloned.1.call-start = ((), (), s32[]{:S(2)}) async-start(), calls=%async_computation.5 | async-start | bytes 28311552 | tf_op jit(solution)/shard_map/reduce_scatter | solution.py:208
  120.1 3.8 copy-start.10
  122.6 1.3 copy-start.8
  123.9 1.2 copy-start.1
  125.1 1.2 copy-start.6
  127.6 1.0 copy-start.2
  150.0 1.2 copy-start.4
  150.0 3.1 copy-start.19
  150.7 2.9 copy-start.17
  171.9 1.4 copy-start.16
  183.3 9.5 %copy-start.3 = (bf16[8,64,8,128]{3,2,1,0:T(8,128)(2,1)S(1)}, bf16[8,64,8,128]{3,2,1,0:T(8,128)(2,1)}, u32[]{:S(2)}) copy-start(bf16[8,64,8,128]{3,2,1,0:T(8,128)(2,1)} %copy-done.2) | copy-start | bytes 3145732
  188.3 42.9 %collective-permute-start = (bf16[512,1024]{1,0:T(8,128)(2,1)}, bf16[512,1024]{1,0:T(8,128)(2,1)}, u32[]{:S(2)}, u32[]{:S(2)}) collective-permute-start(bf16[512,1024]{1,0:T(8,128)(2,1)} %get-tuple-element.57), channel_id=1, source_target_pairs={{0,1},{1,2},{2,3},{3,0},{4,5},{5,6},{6,7},{7,4},{8,9},{9,10},{10,1... | collective-permute-start | bytes 3145736 | tf_op jit(solution)/shard_map/ppermute | solution.py:115
  189.7 72.1 %collective-permute-start.2 = (bf16[512,1024]{1,0:T(8,128)(2,1)}, bf16[512,1024]{1,0:T(8,128)(2,1)}, u32[]{:S(2)}, u32[]{:S(2)}) collective-permute-start(bf16[512,1024]{1,0:T(8,128)(2,1)} %get-tuple-element.58), channel_id=1, source_target_pairs={{0,3},{1,0},{2,1},{3,2},{4,7},{5,4},{6,5},{7,6},{8,11},{9,8},{10,9... | collective-permute-start | bytes 3145736 | tf_op jit(solution)/shard_map/ppermute | solution.py:115
  192.3 11.0 %slice-start = ((s8[8388608]{0:T(1024)(128)(4,1)}), s8[4194304]{0:T(1024)(128)(4,1)S(1)}, s32[]{:S(2)}) async-start(s8[8388608]{0:T(1024)(128)(4,1)} %bitcast.199), calls=%async_computation.7 | async-start | bytes 8388608
  192.3 11.0 %slice-start.1 = ((s8[8388608]{0:T(1024)(128)(4,1)}), s8[4194304]{0:T(1024)(128)(4,1)S(1)}, s32[]{:S(2)}) async-start(s8[8388608]{0:T(1024)(128)(4,1)} %bitcast.199), calls=%async_computation.8 | async-start | bytes 8388608
  192.3 114.1 %collective-permute-start.1 = (bf16[512,1024]{1,0:T(8,128)(2,1)}, bf16[512,1024]{1,0:T(8,128)(2,1)}, u32[]{:S(2)}, u32[]{:S(2)}) collective-permute-start(bf16[512,1024]{1,0:T(8,128)(2,1)} %get-tuple-element.59), channel_id=1, source_target_pairs={{0,2},{1,3},{2,0},{3,1},{4,6},{5,7},{6,4},{7,5},{8,10},{9,11},{10,... | collective-permute-start | bytes 3145736 | tf_op jit(solution)/shard_map/ppermute | solution.py:115
  227.4 83.8 %collective-permute-start.3 = (bf16[512,1024]{1,0:T(8,128)(2,1)}, bf16[512,1024]{1,0:T(8,128)(2,1)}, u32[]{:S(2)}, u32[]{:S(2)}) collective-permute-start(bf16[512,1024]{1,0:T(8,128)(2,1)} %get-tuple-element.54), channel_id=1, source_target_pairs={{0,1},{1,2},{2,3},{3,0},{4,5},{5,6},{6,7},{7,4},{8,9},{9,10},{10,1... | collective-permute-start | bytes 3145736 | tf_op jit(solution)/shard_map/ppermute | solution.py:115
  228.7 82.5 %collective-permute-start.5 = (bf16[512,1024]{1,0:T(8,128)(2,1)S(1)}, bf16[512,1024]{1,0:T(8,128)(2,1)}, u32[]{:S(2)}, u32[]{:S(2)}) collective-permute-start(bf16[512,1024]{1,0:T(8,128)(2,1)S(1)} %get-tuple-element.55), channel_id=1, source_target_pairs={{0,3},{1,0},{2,1},{3,2},{4,7},{5,4},{6,5},{7,6},{8,11},{9,8},{10,9... | collective-permute-start | bytes 3145736 | tf_op jit(solution)/shard_map/ppermute | solution.py:115
  231.2 140.4 %collective-permute-start.4 = (bf16[512,1024]{1,0:T(8,128)(2,1)S(1)}, bf16[512,1024]{1,0:T(8,128)(2,1)}, u32[]{:S(2)}, u32[]{:S(2)}) collective-permute-start(bf16[512,1024]{1,0:T(8,128)(2,1)S(1)} %get-tuple-element.56), channel_id=1, source_target_pairs={{0,2},{1,3},{2,0},{3,1},{4,6},{5,7},{6,4},{7,5},{8,10},{9,11},{10,... | collective-permute-start | bytes 3145736 | tf_op jit(solution)/shard_map/ppermute | solution.py:115
  261.8 109.8 %copy-start.7 = (bf16[512,1024]{1,0:T(8,128)(2,1)S(1)}, bf16[512,1024]{1,0:T(8,128)(2,1)}, u32[]{:S(2)}) copy-start(bf16[512,1024]{1,0:T(8,128)(2,1)} %param.17) | copy-start | bytes 3145732
Sparse Core Ops, SparseCore 0:
  9.5 83.4 all-gather.1
  110.4 32.5 reduce-scatter.3
  146.5 71.3 reduce-scatter.7
  221.3 155.9 reduce-scatter.5
where the time goes:
time: 406 us; the launch traced here: 398 us
  waiting for transfers between devices  161 us (40%)
  matrix products  112 us (28%)
  local copies, waits for them, and re-layouts  43.7 us (11%)
  starting transfers between devices  39.1 us (10%)
  other arithmetic  17.1 us (4%)
  between operations  14.6 us (4%)
  blocking collectives  11 us (3%)
    ppermute x6, waiting for transfers between devices, scatter_sum(): moved = lax.ppermute(block(shift).astype(jnp.bfloat16), axis, ring)  105 us
    all_gather x1, waiting for transfers between devices, per_device(): upstream_full = lax.all_gather(grad_out, 'tp', axis=1, tiled=True)  42.1 us
    dot_general x4, matrix products, back_project(): lax.dot_general(grad_rows, weight, (((1,), (1,)), ((), ())), preferred_el...  39.4 us
    ppermute x6, starting transfers between devices, scatter_sum(): moved = lax.ppermute(block(shift).astype(jnp.bfloat16), axis, ring)  39 us
    dot_general x3, matrix products, project(): jnp.dot(tokens, weight, preferred_element_type=jnp.float32)  23.3 us
    unnamed x76, local copies, waits for them, and re-layouts  22.3 us
    dot_general x1, matrix products, term_maker(): lax.dot_general(tokens, grad_rows, (((0,), (0,)), ((), ())), preferred_el...  18.3 us
    reduce_scatter x1, waiting for transfers between devices, per_device(): lax.psum_scatter(jnp.concatenate([flat_key, flat_value], axis=1), 'ctx',...  12.8 us
  transfers between devices with their start and end apart: 10, of which 4 were waited for; matrix products, arithmetic and copies ran while one was open for 34% of the time, Pallas kernels for 0%

commit v1 on v0

--- a/solution.py
+++ b/solution.py
@@ -163,7 +163,9 @@
     shard_width = summed.shape[1]
     residual = lax.dynamic_slice_in_dim(tokens, lax.axis_index("tp") * shard_width, shard_width, 1)
     output = (residual.astype(jnp.float32) + summed).astype(jnp.bfloat16)
-    upstream_full = lax.all_gather(grad_out, "tp", axis=1, tiled=True)
+    upstream_full = jnp.concatenate(
+        lax.all_to_all(jnp.stack([grad_out] * lax.axis_size("tp")), "tp", 0, 0), axis=1
+    )
     d_attn = back_project(upstream_full, w_out).astype(jnp.bfloat16)
     grads = attend_back(
         query_row_matrix,

time: 406 us -> 423 us (1.042)
  waiting for transfers between devices: 161 us -> 169 us
  starting transfers between devices: 39.1 us -> 45.4 us
    all_to_all x0 -> x1, waiting for transfers between devices: none -> 49.4 us  [per_device(): lax.all_to_all(jnp.stack([grad_out] * lax.axis_size('tp')), 'tp', 0, 0)]
    all_gather x1 -> x0, waiting for transfers between devices: 42.1 us -> none  [per_device(): upstream_full = lax.all_gather(grad_out, 'tp', axis=1, tiled=True)]
    all_to_all x0 -> x1, starting transfers between devices: none -> 6.35 us  [per_device(): lax.all_to_all(jnp.stack([grad_out] * lax.axis_size('tp')), 'tp', 0, 0)]
    unnamed x76 -> x73, local copies, waits for them, and re-layouts: 22.3 us -> 25.4 us
  transfers between devices with their start and end apart: 10 -> 10, of which waited for: 4 -> 5; matrix products, arithmetic and copies ran while one was open for 34% -> 32% of each run, Pallas kernels for 0% -> 0%
where the time goes in v1:
time: 423 us; the launch traced here: 415 us
  waiting for transfers between devices  169 us (40%)
  matrix products  114 us (27%)
  starting transfers between devices  45.4 us (11%)
  local copies, waits for them, and re-layouts  45.2 us (11%)
  other arithmetic  16.9 us (4%)
  between operations  14.5 us (3%)
  blocking collectives  9.52 us (2%)
    ppermute x6, waiting for transfers between devices, scatter_sum(): moved = lax.ppermute(block(shift).astype(jnp.bfloat16), axis, ring)  105 us
    all_to_all x1, waiting for transfers between devices, per_device(): lax.all_to_all(jnp.stack([grad_out] * lax.axis_size('tp')), 'tp', 0, 0)  49.4 us
    dot_general x4, matrix products, back_project(): lax.dot_general(grad_rows, weight, (((1,), (1,)), ((), ())), preferred_el...  39.5 us
    ppermute x6, starting transfers between devices, scatter_sum(): moved = lax.ppermute(block(shift).astype(jnp.bfloat16), axis, ring)  39 us
    dot_general x3, matrix products, project(): jnp.dot(tokens, weight, preferred_element_type=jnp.float32)  25.8 us
    unnamed x73, local copies, waits for them, and re-layouts  25.4 us
    dot_general x1, matrix products, term_maker(): lax.dot_general(tokens, grad_rows, (((0,), (0,)), ((), ())), preferred_el...  20.8 us
    reduce_scatter x1, waiting for transfers between devices, per_device(): lax.psum_scatter(jnp.concatenate([flat_key, flat_value], axis=1), 'ctx',...  13.5 us
  transfers between devices with their start and end apart: 10, of which 5 were waited for; matrix products, arithmetic and copies ran while one was open for 32% of the time, Pallas kernels for 0%

profile of v1, /device:TPU:0, one launch (start us, length us, event | category | flops | bytes accessed | tf_op | source)
XLA Modules:
  0.0 415.0 jit_solution(16406412908146203911)
XLA Ops:
  7.2 1.5 copy.126
  8.7 2.3 stack.2
  11.0 6.3 %all-to-all-start = ((bf16[4,512,1024]{1,2,0:T(8,128)(2,1)}), bf16[4,512,1024]{1,2,0:T(8,128)(2,1)}, u32[]{:S(2)}, u32[]{:S(2)}) async-start(bf16[4,512,1024]{1,2,0:T(8,128)(2,1)} %stack.2), calls=%async_computation | async-start | bytes 8388608 | tf_op jit(solution)/shard_map/all_to_all | solution.py:167
  17.4 9.3 %fusion.14 = bf16[64,8,8,128]{3,1,2,0:T(8,128)(2,1)S(1)} fusion(bf16[512,4096]{1,0:T(8,128)(2,1)} %param.11, bf16[4096,1024]{1,0:T(8,128)(2,1)} %param.12), kind=kOutput, calls=%fused_computation.41 | convolution fusion | flops 4295491584 | bytes 13631488 | tf_op jit(solution)/shard_map/dot_general | solution.py:129
  26.7 7.0 %fusion.15 = bf16[64,8,8,128]{3,1,2,0:T(8,128)(2,1)S(1)} fusion(bf16[512,4096]{1,0:T(8,128)(2,1)S(1)} %copy-done.18, bf16[4096,1024]{1,0:T(8,128)(2,1)} %param.13), kind=kOutput, calls=%fused_computation.42 | convolution fusion | flops 4295491584 | bytes 13631488 | tf_op jit(solution)/shard_map/dot_general | solution.py:129
  34.3 9.5 %fusion.13 = bf16[64,8,8,128]{3,1,2,0:T(8,128)(2,1)S(1)} fusion(bf16[512,4096]{1,0:T(8,128)(2,1)} %param.11, bf16[4096,1024]{1,0:T(8,128)(2,1)} %param.14), kind=kOutput, calls=%fused_computation.40 | convolution fusion | flops 4295491584 | bytes 13631488 | tf_op jit(solution)/shard_map/dot_general | solution.py:129
  44.1 0.9 copy-done.12
  45.1 9.5 %all_gather.3 = bf16[64,2048]{1,0:T(8,128)(2,1)S(1)} all-gather(bf16[8,2048]{1,0:T(8,128)(2,1)S(1)} %pad_maximum_fusion.1), channel_id=1, replica_groups=mesh['ctx'=8,'tp'=4] {'ctx'}, dimensions={0}, use_global_device_ids=true | all-gather | bytes 294912 | tf_op jit(solution)/shard_map/all_gather | solution.py:136
  55.0 1.2 fusion.51
  56.1 0.7 fusion.10
  56.9 0.5 fusion.11
  57.5 0.7 fusion.12
  58.8 0.6 copy-done.13
  59.4 2.1 fusion.29
  61.4 49.4 %all-to-all-done = bf16[4,512,1024]{1,2,0:T(8,128)(2,1)} async-done(((bf16[4,512,1024]{1,2,0:T(8,128)(2,1)}), bf16[4,512,1024]{1,2,0:T(8,128)(2,1)}, u32[]{:S(2)}, u32[]{:S(2)}) %all-to-all-start) | async-done | bytes 4194336 | tf_op jit(solution)/shard_map/all_to_all | solution.py:167
  110.8 9.2 %fusion.16 = bf16[64,8,8,128]{3,1,2,0:T(8,128)(2,1)S(1)} fusion(bf16[512,4096]{0,1:T(8,128)(2,1)} %bitcast.10, bf16[1024,4096]{1,0:T(8,128)(2,1)} %param.15), kind=kOutput, calls=%fused_computation.43 | convolution fusion | flops 4295491584 | bytes 13631488 | tf_op jit(solution)/shard_map/dot_general | solution.py:93
  120.7 0.9 copy-done.11
  121.6 1.1 multiply_reduce_fusion
  122.7 1.9 copy.125
  124.6 1.1 fusion.8
  125.8 1.0 copy-done.4
  127.2 0.9 pad_maximum_fusion
  128.2 9.0 %convolution_convert_fusion = bf16[1024,4096]{1,0:T(8,128)(2,1)} fusion(bf16[512,4096]{0,1:T(8,128)(2,1)} %bitcast.10, bf16[64,8,8,128]{3,2,1,0:T(8,128)(2,1)S(1)} %bitcast.190), kind=kOutput, calls=%fused_computation.2 | convolution fusion | flops 4299161600 | bytes 13631488 | tf_op jit(solution)/shard_map/dot_general | solution.py:216
  137.3 0.7 copy-done.20
  137.9 2.4 fusion.39
  140.4 1.3 copy-done.8
  141.7 1.0 multiply_convert_fusion
  143.4 0.7 copy-done.5
  144.7 0.7 copy.138
  145.4 1.0 copy-done.2
  146.4 1.2 copy.261
  148.1 13.5 %reduce-scatter.4.cloned.1.call-done = f32[8,2048]{1,0:T(8,128)} async-done(((f32[64,2048]{1,0:T(8,128)}), f32[8,2048]{1,0:T(8,128)}) %reduce-scatter.4.cloned.1.call-update) | async-done | bytes 65552 | tf_op jit(solution)/shard_map/reduce_scatter | solution.py:185
  161.5 0.8 slice_bitcast_fusion.4
  162.3 1.7 scatter-add.9
  164.1 1.8 convert_element_type.135
  165.8 0.7 copy.147
  166.6 0.6 scatter-add.6
  167.4 0.7 copy.144
  168.7 0.7 copy-done.17
  169.4 20.8 %convert_bitcast_fusion = bf16[4096,3072]{0,1:T(8,128)(2,1)} fusion(bf16[512,4096]{1,0:T(8,128)(2,1)} %param.11, bf16[512,1024]{1,0:T(8,128)(2,1)S(1)} %bitcast.194, bf16[512,1024]{1,0:T(8,128)(2,1)S(1)} %bitcast.193, bf16[512,1024]{1,0:T(8,128)(2,1)S(1)} %bitcast.192), kind=kOutput, calls=%fused_computation | convolution fusion | flops 12906921984 | bytes 32505856 | tf_op jit(solution)/shard_map/dot_general | solution.py:99
  190.3 1.4 copy-done.16
  191.6 6.9 %fusion.20 = f32[512,4096]{1,0:T(8,128)S(1)} fusion(bf16[1024,4096]{1,0:T(8,128)(2,1)} %param.15, bf16[64,8,8,128]{3,2,1,0:T(8,128)(2,1)S(1)} %bitcast.191), kind=kOutput, calls=%fused_computation.52 | convolution fusion | flops 4294967296 | bytes 17825792 | tf_op jit(solution)/shard_map/dot_general | solution.py:161
  198.5 3.2 copy-done.7
  201.8 1.8 dynamic-slice_convert_fusion.5
  203.6 1.6 collective-permute-start
  205.2 2.4 collective-permute-start.2
  207.6 0.7 collective-permute-start.1
  208.3 10.6 %fusion.48 = f32[512,4096]{1,0:T(8,128)} fusion(bf16[4096,1024]{1,0:T(8,128)(2,1)} %param.12, bf16[64,8,8,128]{3,2,1,0:T(8,128)(2,1)S(1)} %bitcast.181), kind=kOutput, calls=%fused_computation.104 | convolution fusion | flops 4294967296 | bytes 17825792 | tf_op jit(solution)/shard_map/dot_general | solution.py:93
  218.9 6.8 %fusion.49 = f32[512,4096]{1,0:T(8,128)} fusion(bf16[4096,1024]{1,0:T(8,128)(2,1)S(1)} %bitcast.203, bf16[64,8,8,128]{3,2,1,0:T(8,128)(2,1)S(1)} %bitcast.185), kind=kOutput, calls=%fused_computation.105 | convolution fusion | flops 4294967296 | bytes 17825792 | tf_op jit(solution)/shard_map/dot_general | solution.py:93
  225.7 12.9 %add_add_fusion = f32[512,4096]{1,0:T(8,128)} fusion(f32[512,4096]{1,0:T(8,128)} %fusion.48, f32[512,4096]{1,0:T(8,128)} %fusion.49, bf16[4096,1024]{1,0:T(8,128)(2,1)} %param.14, bf16[64,8,8,128]{3,2,1,0:T(8,128)(2,1)S(1)} %bitcast.183), kind=kOutput, calls=%fused_computation.1 | convolution fusion | flops 4299161600 | bytes 34603008 | tf_op jit(solution)/shard_map/dot_general | solution.py:93
  238.6 4.3 %dynamic-slice_convert_fusion.2 = (bf16[512,1024]{1,0:T(8,128)(2,1)}, bf16[512,1024]{1,0:T(8,128)(2,1)S(1)}, bf16[512,1024]{1,0:T(8,128)(2,1)S(1)}) fusion(f32[512,4096]{1,0:T(8,128)} %add_add_fusion, s32[]{:T(128)S(6)} %select_n.64, s32[]{:T(128)S(6)} %select_n.68, s32[]{:T(128)S(6)} %select_n.66), kind=kLoop, calls=%fused_computation.20 | loop fusion | bytes 6291468 | tf_op jit(solution)/shard_map/convert_element_type | solution.py:115
  242.9 1.2 collective-permute-start.3
  244.1 2.6 collective-permute-start.5
  246.7 30.5 %collective-permute-start.4 = (bf16[512,1024]{1,0:T(8,128)(2,1)S(1)}, bf16[512,1024]{1,0:T(8,128)(2,1)}, u32[]{:S(2)}, u32[]{:S(2)}) collective-permute-start(bf16[512,1024]{1,0:T(8,128)(2,1)S(1)} %get-tuple-element.56), channel_id=1, source_target_pairs={{0,2},{1,3},{2,0},{3,1},{4,6},{5,7},{6,4},{7,5},{8,10},{9,11},{10,... | collective-permute-start | bytes 3145736 | tf_op jit(solution)/shard_map/ppermute | solution.py:115
  277.2 44.5 %collective-permute-done.1 = bf16[512,1024]{1,0:T(8,128)(2,1)} collective-permute-done((bf16[512,1024]{1,0:T(8,128)(2,1)}, bf16[512,1024]{1,0:T(8,128)(2,1)}, u32[]{:S(2)}, u32[]{:S(2)}) %collective-permute-start.1) | collective-permute-done | bytes 1048608 | tf_op jit(solution)/shard_map/ppermute | solution.py:115
  321.7 4.7 %add_convert_fusion.1 = bf16[512,1024]{1,0:T(8,128)(2,1)} fusion(bf16[512,1024]{1,0:T(8,128)(2,1)} %collective-permute-done.2, bf16[512,1024]{1,0:T(8,128)(2,1)} %collective-permute-done.1, bf16[512,1024]{1,0:T(8,128)(2,1)S(1)} %collective-permute-done, f32[512,4096]{1,0:T(8,128)} %copy-done.7, s32[]{:T(128)S(6)} %select_n.62, bf16[512,4096]{1,0:T(8,128)(2,1)} %param.11, ...), kind=kLoop, calls=%fused_computation.24 | loop fusion | flops 4718592 | bytes 7340040 | tf_op jit(solution)/shard_map/convert_element_type | solution.py:165
  326.4 60.5 %collective-permute-done.4 = bf16[512,1024]{1,0:T(8,128)(2,1)} collective-permute-done((bf16[512,1024]{1,0:T(8,128)(2,1)S(1)}, bf16[512,1024]{1,0:T(8,128)(2,1)}, u32[]{:S(2)}, u32[]{:S(2)}) %collective-permute-start.4) | collective-permute-done | bytes 1048608 | tf_op jit(solution)/shard_map/ppermute | solution.py:115
  386.9 4.6 %add_convert_fusion = bf16[512,1024]{1,0:T(8,128)(2,1)} fusion(bf16[512,1024]{1,0:T(8,128)(2,1)} %collective-permute-done.5, bf16[512,1024]{1,0:T(8,128)(2,1)} %collective-permute-done.4, bf16[512,1024]{1,0:T(8,128)(2,1)} %collective-permute-done.3, f32[512,4096]{1,0:T(8,128)} %add_add_fusion, s32[]{:T(128)S(6)} %select_n.62, bf16[512,1024]{1,0:T(8,128)(2,1)S(1)} %copy-done.6), kind=kLoop, calls=%fused_computation.17 | loop fusion | flops 4718592 | bytes 7340036 | tf_op jit(solution)/shard_map/convert_element_type | solution.py:208
  391.5 2.9 convert_element_type.147
  394.4 1.5 reduce-scatter.6.cloned.1.call-done
  395.9 4.8 %fusion.50 = (f32[512,1024]{0,1:T(8,128)}, f32[512,1024]{0,1:T(8,128)}, f32[512,1024]{0,1:T(8,128)S(1)}) fusion(bf16[512,3072]{0,1:T(8,128)(2,1)} %reduce-scatter.6.cloned.1.call-done), kind=kLoop, calls=%fused_computation.106 | loop fusion | bytes 12582912 | tf_op jit(solution)/shard_map/slice | solution.py:215
  400.7 2.9 copy.150
  403.6 2.9 copy.149
  406.5 1.8 copy.148
  (94 shorter events, 5.8 us)
Async XLA Ops:
  11.0 99.8 %all-to-all-start = ((bf16[4,512,1024]{1,2,0:T(8,128)(2,1)}), bf16[4,512,1024]{1,2,0:T(8,128)(2,1)}, u32[]{:S(2)}, u32[]{:S(2)}) async-start(bf16[4,512,1024]{1,2,0:T(8,128)(2,1)} %stack.2), calls=%async_computation | async-start | bytes 8388608 | tf_op jit(solution)/shard_map/all_to_all | solution.py:167
  17.4 144.1 %reduce-scatter.4.cloned.1.call-start = ((), (), s32[]{:S(2)}) async-start(), calls=%async_computation.4 | async-start | bytes 589824 | tf_op jit(solution)/shard_map/reduce_scatter | solution.py:185
  17.4 9.3 %copy-start.18 = (bf16[512,4096]{1,0:T(8,128)(2,1)S(1)}, bf16[512,4096]{1,0:T(8,128)(2,1)}, u32[]{:S(2)}) copy-start(bf16[512,4096]{1,0:T(8,128)(2,1)} %param.11) | copy-start | bytes 12582916
  34.3 21.9 %copy-start = (bf16[64,8,8,128]{3,2,1,0:T(8,128)(2,1)}, bf16[64,8,8,128]{3,2,1,0:T(8,128)(2,1)S(1)}, u32[]{:S(2)}) copy-start(bf16[64,8,8,128]{3,2,1,0:T(8,128)(2,1)S(1)} %copy.172) | copy-start | bytes 3145732
  43.8 11.0 %copy-start.25 = (s32[64]{0:T(128)S(1)}, s32[64]{0:T(128)}, u32[]{:S(2)}) copy-start(s32[64]{0:T(128)} %param.16) | copy-start | bytes 772
  44.1 1.0 copy-start.12
  56.8 1.9 copy-start.9
  57.4 1.3 copy-start.19
  58.1 1.2 copy-start.13
  58.2 0.6 copy-start.23
  120.0 1.6 copy-start.11
  122.7 3.1 copy-start.21
  125.8 1.0 copy-start.4
  126.7 1.4 copy-start.15
  128.1 263.4 %reduce-scatter.8.cloned.1.call-start = ((), (), s32[]{:S(2)}) async-start(), calls=%async_computation.6 | async-start | bytes 9437184 | tf_op jit(solution)/shard_map/reduce_scatter | solution.py:219
  137.2 0.8 copy-start.20
  137.2 0.8 copy-start.24
  137.2 4.5 %copy-start.14 = (bf16[64,8,8,128]{3,2,1,0:T(8,128)(2,1)S(1)}, bf16[64,8,8,128]{3,2,1,0:T(8,128)(2,1)}, u32[]{:S(2)}) copy-start(bf16[64,8,8,128]{3,2,1,0:T(8,128)(2,1)} %copy-done.12) | copy-start | bytes 3145732
  137.2 4.5 %copy-start.22 = (f32[8,64,8]{1,2,0:T(8,128)S(1)}, f32[8,64,8]{1,2,0:T(8,128)}, u32[]{:S(2)}) copy-start(f32[8,64,8]{1,2,0:T(8,128)} %copy-done.21) | copy-start | bytes 49156
  137.2 258.7 %reduce-scatter.6.cloned.1.call-start = ((), (), s32[]{:S(2)}) async-start(), calls=%async_computation.5 | async-start | bytes 28311552 | tf_op jit(solution)/shard_map/reduce_scatter | solution.py:210
  137.9 3.8 copy-start.10
  140.4 1.3 copy-start.8
  141.7 1.2 copy-start.1
  142.9 1.2 copy-start.5
  145.4 1.0 copy-start.2
  168.1 1.2 copy-start.17
  190.2 1.4 copy-start.16
  198.5 3.2 copy-start.7
  201.8 6.5 %copy-start.3 = (bf16[8,64,8,128]{3,2,1,0:T(8,128)(2,1)S(1)}, bf16[8,64,8,128]{3,2,1,0:T(8,128)(2,1)}, u32[]{:S(2)}) copy-start(bf16[8,64,8,128]{3,2,1,0:T(8,128)(2,1)} %copy-done.2) | copy-start | bytes 3145732
  203.6 43.2 %collective-permute-start = (bf16[512,1024]{1,0:T(8,128)(2,1)}, bf16[512,1024]{1,0:T(8,128)(2,1)S(1)}, u32[]{:S(2)}, u32[]{:S(2)}) collective-permute-start(bf16[512,1024]{1,0:T(8,128)(2,1)} %get-tuple-element.57), channel_id=1, source_target_pairs={{0,1},{1,2},{2,3},{3,0},{4,5},{5,6},{6,7},{7,4},{8,9},{9,10},{10,1... | collective-permute-start | bytes 3145736 | tf_op jit(solution)/shard_map/ppermute | solution.py:115
  205.2 72.1 %collective-permute-start.2 = (bf16[512,1024]{1,0:T(8,128)(2,1)}, bf16[512,1024]{1,0:T(8,128)(2,1)}, u32[]{:S(2)}, u32[]{:S(2)}) collective-permute-start(bf16[512,1024]{1,0:T(8,128)(2,1)} %get-tuple-element.58), channel_id=1, source_target_pairs={{0,3},{1,0},{2,1},{3,2},{4,7},{5,4},{6,5},{7,6},{8,11},{9,8},{10,9... | collective-permute-start | bytes 3145736 | tf_op jit(solution)/shard_map/ppermute | solution.py:115
  207.6 11.3 %slice-start = ((s8[8388608]{0:T(1024)(128)(4,1)}), s8[4194304]{0:T(1024)(128)(4,1)S(1)}, s32[]{:S(2)}) async-start(s8[8388608]{0:T(1024)(128)(4,1)} %bitcast.202), calls=%async_computation.7 | async-start | bytes 8388608
  207.6 11.3 %slice-start.1 = ((s8[8388608]{0:T(1024)(128)(4,1)}), s8[4194304]{0:T(1024)(128)(4,1)S(1)}, s32[]{:S(2)}) async-start(s8[8388608]{0:T(1024)(128)(4,1)} %bitcast.202), calls=%async_computation.8 | async-start | bytes 8388608
  207.6 114.1 %collective-permute-start.1 = (bf16[512,1024]{1,0:T(8,128)(2,1)}, bf16[512,1024]{1,0:T(8,128)(2,1)}, u32[]{:S(2)}, u32[]{:S(2)}) collective-permute-start(bf16[512,1024]{1,0:T(8,128)(2,1)} %get-tuple-element.59), channel_id=1, source_target_pairs={{0,2},{1,3},{2,0},{3,1},{4,6},{5,7},{6,4},{7,5},{8,10},{9,11},{10,... | collective-permute-start | bytes 3145736 | tf_op jit(solution)/shard_map/ppermute | solution.py:115
  242.9 83.5 %collective-permute-start.3 = (bf16[512,1024]{1,0:T(8,128)(2,1)}, bf16[512,1024]{1,0:T(8,128)(2,1)}, u32[]{:S(2)}, u32[]{:S(2)}) collective-permute-start(bf16[512,1024]{1,0:T(8,128)(2,1)} %get-tuple-element.54), channel_id=1, source_target_pairs={{0,1},{1,2},{2,3},{3,0},{4,5},{5,6},{6,7},{7,4},{8,9},{9,10},{10,1... | collective-permute-start | bytes 3145736 | tf_op jit(solution)/shard_map/ppermute | solution.py:115
  244.1 82.3 %collective-permute-start.5 = (bf16[512,1024]{1,0:T(8,128)(2,1)S(1)}, bf16[512,1024]{1,0:T(8,128)(2,1)}, u32[]{:S(2)}, u32[]{:S(2)}) collective-permute-start(bf16[512,1024]{1,0:T(8,128)(2,1)S(1)} %get-tuple-element.55), channel_id=1, source_target_pairs={{0,3},{1,0},{2,1},{3,2},{4,7},{5,4},{6,5},{7,6},{8,11},{9,8},{10,9... | collective-permute-start | bytes 3145736 | tf_op jit(solution)/shard_map/ppermute | solution.py:115
  246.7 140.2 %collective-permute-start.4 = (bf16[512,1024]{1,0:T(8,128)(2,1)S(1)}, bf16[512,1024]{1,0:T(8,128)(2,1)}, u32[]{:S(2)}, u32[]{:S(2)}) collective-permute-start(bf16[512,1024]{1,0:T(8,128)(2,1)S(1)} %get-tuple-element.56), channel_id=1, source_target_pairs={{0,2},{1,3},{2,0},{3,1},{4,6},{5,7},{6,4},{7,5},{8,10},{9,11},{10,... | collective-permute-start | bytes 3145736 | tf_op jit(solution)/shard_map/ppermute | solution.py:115
  277.2 109.7 %copy-start.6 = (bf16[512,1024]{1,0:T(8,128)(2,1)S(1)}, bf16[512,1024]{1,0:T(8,128)(2,1)}, u32[]{:S(2)}) copy-start(bf16[512,1024]{1,0:T(8,128)(2,1)} %param.17) | copy-start | bytes 3145732
Sparse Core Ops, SparseCore 0:
  128.2 33.2 reduce-scatter.3
  165.0 71.2 reduce-scatter.7
  239.9 155.9 reduce-scatter.5
